TPU v7x, 32 devices: a whole 2x2x4 slice. The times are simulated.
32 devices in a mesh: groups: 2 (over y), rows: 4 (over z), cols: 2 (over x), sub: 2 (over core).
Axes of the slice: x: 2, y: 2, z: 4, core: 2. Of those that a mesh axis runs over, the one named last changes fastest.
Arguments:
- tile_index: int32 [64, 2], P(('groups', 'rows', 'cols', 'sub')), parts along dimension 0, may hold values from 0 to 7, as said below
- tile_values: bfloat16 [64, 256, 256], P(('groups', 'rows', 'cols', 'sub')), parts along dimension 0, may hold values from -0.125 to 0.125
- onsite_energy: float32 [4096], P(('groups', 'rows', 'cols')), parts along dimension 0, may hold values from 0.5 to 4
- start_block: float32 [4096, 64], P(('groups', 'rows', 'cols')), parts along dimension 0, may hold values from -6 to 6
- previous_block: float32 [4096, 64], P(('groups', 'rows', 'cols')), parts along dimension 0, may hold values from -6 to 6
- previous_coupling: float32 [128, 64], P('groups'), parts along dimension 0, may hold values from -0.6 to 0.6
- stored_basis: float32 [8, 4096, 64], P('sub', ('groups', 'rows', 'cols')), parts along dimension 1, may hold values from -6 to 6
Outputs:
- new_blocks: float32 [1, 4096, 64], P(None, ('groups', 'rows', 'cols')), parts along dimension 1
- diagonal_blocks: float32 [1, 128, 64], P(None, 'groups'), parts along dimension 1
- coupling_blocks: float32 [1, 128, 64], P(None, 'groups'), parts along dimension 1
There are 2 independent parts, one for each index of `groups`. A program takes and returns all parts, laid end to end along the dimension named above; each array names one. Nothing has to cross between parts.
Inputs may be any that keep to these rules, and one draw needn't show every extreme that they name: `tile_index`: tile rows of a device's tiles lie in the rows of the operator that the device's index of rows and cols holds; tile columns lie in the rows held by some index of rows with the same index of cols. Tiles may repeat.
All inputs are finite; a program needn't handle non-finite values.
Results may differ from a plain program's by a relative error of at most 0.0019.
Values may be sent and summed in bfloat16 or wider, within the bound.
A program may use at most 64 MiB of HBM per device.

v0:
```python
import jax
import jax.numpy as jnp
from jax import lax
from jax.sharding import PartitionSpec as P

BLOCK = 64
TILE = 256
highest = lax.Precision.HIGHEST


def apply_operator(tile_index, tile_values, onsite_energy, current):
    local_rows = current.shape[0]
    tile_rows = local_rows // TILE
    band_count = lax.axis_size("rows")
    column_count = lax.axis_size("cols")
    narrow = current.astype(jnp.bfloat16)
    own_tiles = narrow.reshape(tile_rows, TILE, BLOCK)
    local_row = tile_index[:, 0] % tile_rows
    column = tile_index[:, 1]
    source = column // tile_rows // column_count * tile_rows + column % tile_rows
    gathered = lax.all_gather(own_tiles, "rows", axis=0, tiled=True)
    pulled = jnp.einsum(
        "kab,kbn->kan", tile_values, gathered[source], preferred_element_type=jnp.float32
    )
    pushed = jnp.einsum(
        "kab,kan->kbn", tile_values, own_tiles[local_row], preferred_element_type=jnp.float32
    )
    slot_count = band_count * tile_rows
    slot_range = jnp.arange(slot_count, dtype=jnp.int32)
    push_onehot = (source[None, :] == slot_range[:, None]).astype(jnp.float32)
    terms = jnp.einsum("sk,kbn->sbn", push_onehot, pushed, precision=highest)
    received = lax.psum_scatter(terms, "rows", scatter_dimension=0, tiled=True)
    row_onehot = (local_row[None, :] == jnp.arange(tile_rows, dtype=jnp.int32)[:, None]).astype(
        jnp.float32
    )
    partial_total = received + jnp.einsum("tk,kan->tan", row_onehot, pulled, precision=highest)
    total = lax.psum(partial_total, "sub")
    return total.reshape(local_rows, BLOCK) + onsite_energy[:, None] * current


def local(
    tile_index,
    tile_values,
    onsite_energy,
    start_block,
    previous_block,
    previous_coupling,
    stored_basis,
):
    local_rows = start_block.shape[0]
    total_rows = local_rows * lax.axis_size("rows") * lax.axis_size("cols")
    coupling = jnp.triu(previous_coupling)
    correlation_local = jnp.einsum("kib,ic->kbc", stored_basis, start_block, precision=highest)
    correlation = lax.psum(correlation_local, ("rows", "cols")) / total_rows
    images = apply_operator(tile_index, tile_values, onsite_energy, start_block)
    images = images - jnp.dot(previous_block, coupling.T, precision=highest)
    diagonal_local = jnp.dot(start_block.T, images, precision=highest)
    stored_local = jnp.einsum("kib,ic->kbc", stored_basis, images, precision=highest)
    raw_diagonal, raw_stored = lax.psum((diagonal_local, stored_local), ("rows", "cols"))
    diagonal = raw_diagonal / total_rows
    projection = raw_stored / total_rows - jnp.einsum(
        "kbc,cd->kbd", correlation, diagonal, precision=highest
    )
    images = images - jnp.dot(start_block, diagonal, precision=highest)
    removal_local = jnp.einsum("kib,kbc->ic", stored_basis, projection, precision=highest)
    removal = lax.psum(removal_local, "sub")
    images = images - removal
    gram_local = jnp.dot(images.T, images, precision=highest)
    gram = lax.psum(gram_local, ("rows", "cols")) / total_rows
    lower_factor = jnp.linalg.cholesky(gram)
    following = lax.linalg.triangular_solve(
        lower_factor, images, left_side=False, lower=True, transpose_a=True
    )
    new_list = [following]
    diagonal_list = [diagonal]
    coupling_list = [lower_factor.T]
    return (jnp.stack(new_list), jnp.stack(diagonal_list), jnp.stack(coupling_list))


def solution(mesh):
    return jax.shard_map(
        local,
        mesh=mesh,
        in_specs=(
            P(("groups", "rows", "cols", "sub"), None),
            P(("groups", "rows", "cols", "sub"), None, None),
            P(("groups", "rows", "cols")),
            P(("groups", "rows", "cols"), None),
            P(("groups", "rows", "cols"), None),
            P("groups", None),
            P("sub", ("groups", "rows", "cols"), None),
        ),
        out_specs=(
            P(None, ("groups", "rows", "cols"), None),
            P(None, "groups", None),
            P(None, "groups", None),
        ),
        check_vma=False,
    )
```

profile of v0, /device:TPU:0, one launch (start us, length us, event | category | flops | bytes accessed | tf_op | source)
XLA Modules:
  0.0 217.6 jit_solution(17785886655713540770)
XLA Ops:
  7.2 0.9 convert_element_type.2
  8.1 0.9 fusion.27
  9.0 0.2 fusion.15
  9.2 0.5 fusion.5
  9.7 0.8 copy.31
  10.6 15.6 %all-gather = bf16[1024,64]{0,1:T(8,128)(2,1)S(1)} all-gather(bf16[256,64]{0,1:T(8,128)(2,1)S(1)} %convert_element_type.2), channel_id=2, replica_groups=mesh['groups'=2,'rows'=4,'cols'=2,'sub'=2] {'rows'}, dimensions={0}, use_global_device_ids=true | all-gather | bytes 163840 | tf_op jit(solution)/shard_map/all_gather | solution.py:21
  26.2 0.6 gather_fusion
  26.8 0.2 convolution_bitcast_fusion.1
  27.0 9.0 %fusion.3 = f32[1,256,64]{0,1,2:T(8,128)} fusion(f32[2,256,64]{1,2,0:T(8,128)S(1)} %convolution_bitcast_fusion.1), kind=kOutput, calls=%fused_computation.13 | convolution fusion | flops 393216 | bytes 196608 | tf_op jit(solution)/shard_map/tk,kan->tan/dot_general | solution.py:36
  36.0 5.2 %copy.42 = f32[1,256,64]{1,2,0:T(8,128)S(1)} copy(f32[1,256,64]{0,1,2:T(8,128)} %fusion.3) | data formatting | bytes 131072 | tf_op jit(solution)/shard_map/tk,kan->tan/dot_general | solution.py:36
  41.2 1.2 fusion.8
  42.4 1.5 add_bitcast_fusion
  43.9 18.8 %all-reduce.5.cloned.1.call-done = f32[256,64]{0,1:T(8,128)} async-done(((f32[256,64]{0,1:T(8,128)}), f32[256,64]{0,1:T(8,128)}) %all-reduce.5.cloned.1.call-update) | async-done | bytes 65552 | tf_op jit(solution)/shard_map/psum | solution.py:37
  62.8 1.1 fusion.2
  63.9 1.2 convolution_bitcast_fusion
  65.1 0.2 convolution_bitcast_fusion.6
  65.3 37.4 %psum.43 = f32[64,64]{0,1:T(8,128)S(1)} all-reduce(f32[64,64]{0,1:T(8,128)S(1)} %convolution_bitcast_fusion.6), channel_id=1, replica_groups=mesh['groups'=2,'rows'=4,'cols'=2,'sub'=2] {'rows','cols'}, use_global_device_ids=true, to_apply=%region_2.3 | all-reduce | flops 4096 | bytes 32768 | tf_op jit(solution)/shard_map/psum | solution.py:59
  102.7 36.2 %all-reduce.9.cloned.1.call-done = (f32[4,64,64]{1,2,0:T(8,128)}, f32[4,64,64]{1,2,0:T(8,128)}) async-done(((f32[4,64,64]{1,2,0:T(8,128)}, f32[4,64,64]{1,2,0:T(8,128)}), (f32[4,64,64]{1,2,0:T(8,128)}, f32[4,64,64]{1,2,0:T(8,128)})) %all-reduce.9.cloned.1.call-update) | async-done | bytes 131088 | tf_op jit(solution)/shard_map/psum | solution.py:54
  138.9 1.2 convolution_subtract_fusion
  140.1 0.9 convolution_bitcast_fusion.5
  141.1 0.7 copy.39
  141.8 16.8 %all-reduce.7.cloned.1.call-done = f32[256,64]{0,1:T(8,128)} async-done(((f32[256,64]{0,1:T(8,128)}), f32[256,64]{0,1:T(8,128)}) %all-reduce.7.cloned.1.call-update) | async-done | bytes 65552 | tf_op jit(solution)/shard_map/psum | solution.py:66
  158.6 1.0 fusion.1
  159.7 0.2 fusion.35
  159.9 37.4 %psum.47 = f32[64,64]{0,1:T(8,128)S(1)} all-reduce(f32[64,64]{0,1:T(8,128)S(1)} %fusion.35), channel_id=1, replica_groups=mesh['groups'=2,'rows'=4,'cols'=2,'sub'=2] {'rows','cols'}, use_global_device_ids=true, to_apply=%region_6.7 | all-reduce | flops 4096 | bytes 32768 | tf_op jit(solution)/shard_map/psum | solution.py:69
  197.3 0.1 copy.38
  197.4 5.8 %cholesky.15 = f32[64,64]{1,0:T(8,128)S(1)} custom-call(f32[64,64]{1,0:T(8,128)S(1)} %fusion.13), custom_call_target="Cholesky" | custom-call | tf_op jit(solution)/shard_map/jit(cholesky)/cholesky | solution.py:70
  203.3 0.6 compare_reduce_fusion
  203.9 0.7 fusion.20
  204.6 4.9 %custom-call.6 = f32[1,64,64]{1,2,0:T(8,128)S(1)} custom-call(f32[1,64,64]{2,1,0:T(8,128)S(1)} %get-tuple-element.20), custom_call_target="InvertDiagBlocksLowerTriangular" | custom-call | tf_op jit(solution)/shard_map/triangular_solve | solution.py:71
  209.5 0.9 convolution_bitcast_fusion.2
  210.4 0.7 copy.40
  (29 shorter events, 0.4 us)
Async XLA Ops:
  7.2 1.9 copy-start
  7.2 35.2 %reduce-scatter.2.cloned.1.call-start = ((), (), s32[]{:S(2)}) async-start(), calls=%async_computation.1 | async-start | bytes 327680 | tf_op jit(solution)/shard_map/reduce_scatter | solution.py:32
  10.5 52.2 %all-reduce.5.cloned.1.call-start = ((), (), s32[]{:S(2)}) async-start(), calls=%async_computation.2 | async-start | bytes 131072 | tf_op jit(solution)/shard_map/psum | solution.py:37
  27.0 14.2 %copy-start.1 = (f32[4,256,64]{1,2,0:T(8,128)S(1)}, f32[4,256,64]{1,2,0:T(8,128)}, u32[]{:S(2)}) copy-start(f32[4,256,64]{1,2,0:T(8,128)} %param.13) | copy-start | bytes 786436
  27.0 14.2 %copy-start.2 = (f32[256,64]{0,1:T(8,128)S(1)}, f32[256,64]{0,1:T(8,128)}, u32[]{:S(2)}) copy-start(f32[256,64]{0,1:T(8,128)} %param.10) | copy-start | bytes 196612
  27.0 35.8 %copy-start.3 = (f32[256,64]{0,1:T(8,128)S(1)}, f32[256,64]{0,1:T(8,128)}, u32[]{:S(2)}) copy-start(f32[256,64]{0,1:T(8,128)} %param.11) | copy-start | bytes 196612
  27.0 35.7 %copy-start.4 = (f32[64,64]{1,0:T(8,128)S(1)}, f32[64,64]{1,0:T(8,128)}, u32[]{:S(2)}) copy-start(f32[64,64]{1,0:T(8,128)} %param.12) | copy-start | bytes 49156
  27.0 35.7 %copy-start.5 = (f32[256]{0:T(256)S(1)}, f32[256]{0:T(256)}, u32[]{:S(2)}) copy-start(f32[256]{0:T(256)} %param.9) | copy-start | bytes 3076
  43.9 95.0 %all-reduce.9.cloned.1.call-start = ((), (), s32[]{:S(2)}) async-start(), calls=%async_computation.4 | async-start | bytes 524288 | tf_op jit(solution)/shard_map/psum | solution.py:54
  65.0 93.6 %all-reduce.7.cloned.1.call-start = ((), (), s32[]{:S(2)}) async-start(), calls=%async_computation.3 | async-start | bytes 131072 | tf_op jit(solution)/shard_map/psum | solution.py:66
Sparse Core Ops, SparseCore 0:
  10.6 22.8 reduce-scatter.1
  44.0 18.7 all-reduce.4
  66.2 72.6 all-reduce.8
  141.6 16.9 all-reduce.6
where the time goes:
time: 218 us
  blocking collectives  90.4 us (41%)
  waiting for transfers between devices  71.9 us (33%)
  matrix products  17.8 us (8%)
  other arithmetic  15.4 us (7%)
  between operations  13.9 us (6%)
  local copies, waits for them, and re-layouts  8.02 us (4%)
    psum x1, blocking collectives, local(): gram = lax.psum(gram_local, ('rows', 'cols')) / total_rows  37.4 us
    psum x1, blocking collectives, local(): lax.psum((diagonal_local, stored_local), ('rows', 'cols'))  37.4 us
    psum x1, waiting for transfers between devices, local(): correlation = lax.psum(correlation_local, ('rows', 'cols')) / total_rows  36.2 us
    psum x1, waiting for transfers between devices, apply_operator(): total = lax.psum(partial_total, 'sub')  18.8 us
    psum x1, waiting for transfers between devices, local(): removal = lax.psum(removal_local, 'sub')  16.8 us
    all_gather x1, blocking collectives, apply_operator(): gathered = lax.all_gather(own_tiles, 'rows', axis=0, tiled=True)  15.6 us
    dot_general x1, matrix products, apply_operator(): jnp.einsum('tk,kan->tan', row_onehot, pulled, precision=highest)  8.95 us
    another operation x3, other arithmetic, local(): lower_factor = jnp.linalg.cholesky(gram)  6.52 us
  transfers between devices with their start and end apart: 4, of which 3 were waited for; matrix products, arithmetic and copies ran while one was open for 8% of the time, Pallas kernels for 0%

commit v1 on v0

--- a/solution.py
+++ b/solution.py
@@ -63,7 +63,7 @@
     )
     images = images - jnp.dot(start_block, diagonal, precision=highest)
     removal_local = jnp.einsum("kib,kbc->ic", stored_basis, projection, precision=highest)
-    removal = lax.psum(removal_local, "sub")
+    removal = jnp.sum(lax.all_gather(removal_local, "sub"), axis=0)
     images = images - removal
     gram_local = jnp.dot(images.T, images, precision=highest)
     gram = lax.psum(gram_local, ("rows", "cols")) / total_rows

time: 218 us -> 232 us (1.064)
  waiting for transfers between devices: 71.9 us -> 86.9 us
    psum x1, waiting for transfers between devices: 36.2 us -> 68 us  [local(): correlation = lax.psum(correlation_local, ('rows', 'cols')) / total_rows]
    psum x1 -> x0, waiting for transfers between devices: 16.8 us -> none  [local(): removal = lax.psum(removal_local, 'sub')]
  transfers between devices with their start and end apart: 4 -> 3, of which waited for: 3 -> 2; matrix products, arithmetic and copies ran while one was open for 8% -> 7% of each run, Pallas kernels for 0% -> 0%
where the time goes in v1:
time: 232 us; the launch traced here: 231 us
  blocking collectives  90.3 us (39%)
  waiting for transfers between devices  86.9 us (37%)
  matrix products  16.3 us (7%)
  other arithmetic  15.5 us (7%)
  between operations  13.9 us (6%)
  local copies, waits for them, and re-layouts  8.11 us (3%)
    psum x1, waiting for transfers between devices, local(): correlation = lax.psum(correlation_local, ('rows', 'cols')) / total_rows  68 us
    psum x1, blocking collectives, local(): lax.psum((diagonal_local, stored_local), ('rows', 'cols'))  37.4 us
    psum x1, blocking collectives, local(): gram = lax.psum(gram_local, ('rows', 'cols')) / total_rows  35.4 us
    psum x1, waiting for transfers between devices, apply_operator(): total = lax.psum(partial_total, 'sub')  18.8 us
    all_gather x1, blocking collectives, apply_operator(): gathered = lax.all_gather(own_tiles, 'rows', axis=0, tiled=True)  15.6 us
    dot_general x1, matrix products, apply_operator(): jnp.einsum('tk,kan->tan', row_onehot, pulled, precision=highest)  8.95 us
    another operation x3, other arithmetic, local(): lower_factor = jnp.linalg.cholesky(gram)  6.52 us
    dot_general x1, local copies, waits for them, and re-layouts, apply_operator(): jnp.einsum('tk,kan->tan', row_onehot, pulled, precision=highest)  5.19 us
  transfers between devices with their start and end apart: 3, of which 2 were waited for; matrix products, arithmetic and copies ran while one was open for 7% of the time, Pallas kernels for 0%

profile of v1, /device:TPU:0, one launch (start us, length us, event | category | flops | bytes accessed | tf_op | source)
XLA Modules:
  0.0 231.2 jit_solution(10343153231105846824)
XLA Ops:
  7.2 0.9 convert_element_type.2
  8.1 0.9 fusion.27
  9.0 0.2 fusion.15
  9.2 0.5 fusion.5
  9.7 0.8 copy.31
  10.6 15.6 %all-gather = bf16[1024,64]{0,1:T(8,128)(2,1)S(1)} all-gather(bf16[256,64]{0,1:T(8,128)(2,1)S(1)} %convert_element_type.2), channel_id=2, replica_groups=mesh['groups'=2,'rows'=4,'cols'=2,'sub'=2] {'rows'}, dimensions={0}, use_global_device_ids=true | all-gather | bytes 163840 | tf_op jit(solution)/shard_map/all_gather | solution.py:21
  26.2 0.6 gather_fusion
  26.8 0.2 convolution_bitcast_fusion.1
  27.0 9.0 %fusion.3 = f32[1,256,64]{0,1,2:T(8,128)} fusion(f32[2,256,64]{1,2,0:T(8,128)S(1)} %convolution_bitcast_fusion.1), kind=kOutput, calls=%fused_computation.13 | convolution fusion | flops 393216 | bytes 196608 | tf_op jit(solution)/shard_map/tk,kan->tan/dot_general | solution.py:36
  36.0 5.2 %copy.42 = f32[1,256,64]{1,2,0:T(8,128)S(1)} copy(f32[1,256,64]{0,1,2:T(8,128)} %fusion.3) | data formatting | bytes 131072 | tf_op jit(solution)/shard_map/tk,kan->tan/dot_general | solution.py:36
  41.2 1.2 fusion.8
  42.4 1.5 add_bitcast_fusion
  43.9 18.8 %all-reduce.4.cloned.1.call-done = f32[256,64]{0,1:T(8,128)} async-done(((f32[256,64]{0,1:T(8,128)}), f32[256,64]{0,1:T(8,128)}) %all-reduce.4.cloned.1.call-update) | async-done | bytes 65552 | tf_op jit(solution)/shard_map/psum | solution.py:37
  62.8 1.1 fusion.2
  63.9 0.2 convolution_bitcast_fusion.6
  64.1 1.2 convolution_bitcast_fusion
  65.2 37.4 %psum.36 = f32[64,64]{0,1:T(8,128)S(1)} all-reduce(f32[64,64]{0,1:T(8,128)S(1)} %convolution_bitcast_fusion.6), channel_id=1, replica_groups=mesh['groups'=2,'rows'=4,'cols'=2,'sub'=2] {'rows','cols'}, use_global_device_ids=true, to_apply=%region_2.3 | all-reduce | flops 4096 | bytes 32768 | tf_op jit(solution)/shard_map/psum | solution.py:59
  102.7 0.7 copy.39
  103.4 68.0 %all-reduce.6.cloned.1.call-done = (f32[4,64,64]{1,2,0:T(8,128)}, f32[4,64,64]{1,2,0:T(8,128)}) async-done(((f32[4,64,64]{1,2,0:T(8,128)}, f32[4,64,64]{1,2,0:T(8,128)}), (f32[4,64,64]{1,2,0:T(8,128)}, f32[4,64,64]{1,2,0:T(8,128)})) %all-reduce.6.cloned.1.call-update) | async-done | bytes 131088 | tf_op jit(solution)/shard_map/psum | solution.py:54
  171.4 1.2 convolution_subtract_fusion
  172.6 0.3 convolution_bitcast_fusion.5
  172.9 1.9 all-gather.1
  174.9 0.2 reduce_sum.9
  175.1 0.2 fusion.1
  175.3 0.2 fusion.35
  175.5 35.4 %psum.39 = f32[64,64]{0,1:T(8,128)S(1)} all-reduce(f32[64,64]{0,1:T(8,128)S(1)} %fusion.35), channel_id=1, replica_groups=mesh['groups'=2,'rows'=4,'cols'=2,'sub'=2] {'rows','cols'}, use_global_device_ids=true, to_apply=%region_6.7 | all-reduce | flops 4096 | bytes 32768 | tf_op jit(solution)/shard_map/psum | solution.py:69
  211.0 5.8 %cholesky.15 = f32[64,64]{1,0:T(8,128)S(1)} custom-call(f32[64,64]{1,0:T(8,128)S(1)} %fusion.13), custom_call_target="Cholesky" | custom-call | tf_op jit(solution)/shard_map/jit(cholesky)/cholesky | solution.py:70
  216.9 0.6 compare_reduce_fusion
  217.6 0.7 fusion.20
  218.2 4.9 %custom-call.6 = f32[1,64,64]{1,2,0:T(8,128)S(1)} custom-call(f32[1,64,64]{2,1,0:T(8,128)S(1)} %get-tuple-element.20), custom_call_target="InvertDiagBlocksLowerTriangular" | custom-call | tf_op jit(solution)/shard_map/triangular_solve | solution.py:71
  223.1 0.9 convolution_bitcast_fusion.2
  224.0 0.7 copy.40
  (29 shorter events, 0.5 us)
Async XLA Ops:
  7.2 1.9 copy-start
  7.2 35.2 %reduce-scatter.2.cloned.1.call-start = ((), (), s32[]{:S(2)}) async-start(), calls=%async_computation.1 | async-start | bytes 327680 | tf_op jit(solution)/shard_map/reduce_scatter | solution.py:32
  10.5 52.2 %all-reduce.4.cloned.1.call-start = ((), (), s32[]{:S(2)}) async-start(), calls=%async_computation.2 | async-start | bytes 131072 | tf_op jit(solution)/shard_map/psum | solution.py:37
  27.0 14.2 %copy-start.1 = (f32[4,256,64]{1,2,0:T(8,128)S(1)}, f32[4,256,64]{1,2,0:T(8,128)}, u32[]{:S(2)}) copy-start(f32[4,256,64]{1,2,0:T(8,128)} %param.13) | copy-start | bytes 786436
  27.0 14.2 %copy-start.2 = (f32[256,64]{0,1:T(8,128)S(1)}, f32[256,64]{0,1:T(8,128)}, u32[]{:S(2)}) copy-start(f32[256,64]{0,1:T(8,128)} %param.10) | copy-start | bytes 196612
  27.0 35.8 %copy-start.3 = (f32[256,64]{0,1:T(8,128)S(1)}, f32[256,64]{0,1:T(8,128)}, u32[]{:S(2)}) copy-start(f32[256,64]{0,1:T(8,128)} %param.11) | copy-start | bytes 196612
  27.0 35.7 %copy-start.4 = (f32[64,64]{1,0:T(8,128)S(1)}, f32[64,64]{1,0:T(8,128)}, u32[]{:S(2)}) copy-start(f32[64,64]{1,0:T(8,128)} %param.12) | copy-start | bytes 49156
  27.0 35.7 %copy-start.5 = (f32[256]{0:T(256)S(1)}, f32[256]{0:T(256)}, u32[]{:S(2)}) copy-start(f32[256]{0:T(256)} %param.9) | copy-start | bytes 3076
  43.9 127.5 %all-reduce.6.cloned.1.call-start = ((), (), s32[]{:S(2)}) async-start(), calls=%async_computation.3 | async-start | bytes 524288 | tf_op jit(solution)/shard_map/psum | solution.py:54
Sparse Core Ops, SparseCore 0:
  10.6 22.8 reduce-scatter.1
  44.0 18.7 all-reduce.3
  102.8 68.5 all-reduce.5
